TPU v7x, 32 devices: a whole 2x2x4 slice. The times are simulated.
32 devices in a mesh: dp: 8 (over z, core), tp: 4 (over y, x).
Axes of the slice: x: 2, y: 2, z: 4, core: 2. Of those that a mesh axis runs over, the one named last changes fastest.
Arguments:
- hidden_states: bfloat16 [2048, 3584], P('dp'), may hold values from -21 to 21
- resp_lengths: int32 [4], replicated, may hold values from 1 to 1280, 2048 in all
- w_query: bfloat16 [3584, 512], P('dp', 'tp'), may hold values from -0.25 to 0.25
- w_keyval: bfloat16 [3584, 1024], P('dp', 'tp'), may hold values from -0.09375 to 0.09375
- w_out: bfloat16 [512, 3584], P('tp', 'dp'), may hold values from -0.25 to 0.25
Outputs:
- attended: bfloat16 [2048, 3584], P('dp', 'tp')
Inputs may be any that keep to these rules, and one draw needn't show every extreme that they name: `resp_lengths`: the 4 lengths sum to 2048; the longest is exactly 1280.
All inputs are finite; a program needn't handle non-finite values.
Results may differ from a plain program's by a relative error of at most 0.015.
The roundings to bfloat16 on the way count: a program that leaves them out, or rounds other values in their place, can miss the bound.
Values may be sent and summed in bfloat16 or wider, within the bound.
No kernel may reach another device: no remote copies, remote signals or barrier semaphores. Data moves between devices by JAX's collectives and lax.ppermute only.
A program may use at most 64 MiB of HBM per device.

v0:
```python
import jax
import jax.numpy as jnp
from jax import lax
from jax.sharding import PartitionSpec as P

HD = 128


def segment_of(position, resp_ends):
    return jnp.sum(
        (position[:, None] >= resp_ends[None, :]).astype(jnp.int32), axis=1, dtype=jnp.int32
    )


def body(hidden_states, resp_lengths, w_query, w_keyval, w_out):
    token_rows = hidden_states.shape[0]
    head_scale = HD ** (-0.5)
    pieces = (
        lax.all_gather(w_query, "dp", axis=0, tiled=True),
        lax.all_gather(w_keyval, "dp", axis=0, tiled=True),
    )
    query_sum = jnp.dot(hidden_states, pieces[0], preferred_element_type=jnp.float32)
    keyval_sum = jnp.dot(hidden_states, pieces[1], preferred_element_type=jnp.float32)
    query = (query_sum * head_scale).astype(jnp.bfloat16)
    keyval = lax.all_gather(keyval_sum.astype(jnp.bfloat16), "tp", axis=1, tiled=True)
    kv_count = keyval.shape[1] // (2 * HD)
    per_group = lax.axis_size("tp") // kv_count
    kv_head = lax.axis_index("tp") // per_group
    key_head = lax.dynamic_slice_in_dim(keyval, kv_head * HD, HD, 1)
    value_head = lax.dynamic_slice_in_dim(keyval, (kv_count + kv_head) * HD, HD, 1)
    head_pair = jnp.concatenate([key_head, value_head], axis=1)
    resp_ends = jnp.cumsum(resp_lengths, dtype=jnp.int32)
    own_begin = lax.axis_index("dp") * token_rows
    query_pos = own_begin + jnp.arange(token_rows, dtype=jnp.int32)
    query_seg = segment_of(query_pos, resp_ends)
    pieces = lax.all_gather(head_pair, "dp", axis=0, tiled=True)
    largest = jnp.full((token_rows,), -1e30, jnp.float32)
    height = pieces.shape[0]
    key_pos = jnp.arange(height, dtype=jnp.int32)
    key_seg = segment_of(key_pos, resp_ends)
    scores = jnp.dot(query, pieces[:, :HD].T, preferred_element_type=jnp.float32)
    allowed = (
        (query_seg[:, None] == key_seg[None, :])
        & (key_pos[None, :] <= query_pos[:, None])
        & (key_pos[None, :] >= 0)
    )
    newest = jnp.maximum(largest, jnp.max(jnp.where(allowed, scores, jnp.float32(-1e30)), axis=1))
    expw = jnp.where(allowed, jnp.exp(scores - newest[:, None]), jnp.float32(0.0))
    denom = jnp.sum(expw, axis=1)
    numer = jnp.dot(expw.astype(jnp.bfloat16), pieces[:, HD:], preferred_element_type=jnp.float32)
    heads_out = (numer / denom[:, None]).astype(jnp.bfloat16)
    terms = jnp.dot(
        heads_out,
        lax.all_gather(w_out, "dp", axis=1, tiled=True),
        preferred_element_type=jnp.float32,
    )
    summed = lax.psum_scatter(terms.astype(jnp.bfloat16), "tp", scatter_dimension=1, tiled=True)
    return summed


def solution(mesh):
    return jax.shard_map(
        body,
        mesh=mesh,
        in_specs=(P("dp", None), P(), P("dp", "tp"), P("dp", "tp"), P("tp", "dp")),
        out_specs=P("dp", "tp"),
        check_vma=False,
    )
```

profile of v0, /device:TPU:0, one launch (start us, length us, event | category | flops | bytes accessed | tf_op | source)
XLA Modules:
  0.0 146.7 jit_solution(7602217867818827257)
XLA Ops:
  6.5 0.0 copy-start
  6.5 0.0 all-gather.3.cloned.1.call-start
  6.5 0.7 all-gather.3.cloned.1.call-update
  7.3 0.0 all-gather.5.cloned.1.call-start
  7.3 0.0 copy-start.3
  7.3 0.0 copy-start.1
  7.3 31.4 %all-gather.3.cloned.1.call-done = bf16[3584,256]{1,0:T(8,128)(2,1)} async-done(((bf16[448,256]{1,0:T(8,128)(2,1)}), bf16[3584,256]{1,0:T(8,128)(2,1)}) %all-gather.3.cloned.1.call-update) | async-done | bytes 1835024 | tf_op jit(solution)/shard_map/all_gather | solution.py:20
  38.7 0.0 copy-done
  38.7 2.1 %convolution_convert_fusion.1 = bf16[256,256]{1,0:T(8,128)(2,1)S(1)} fusion(bf16[256,3584]{1,0:T(8,128)(2,1)S(1)} %copy-done, bf16[3584,256]{1,0:T(8,128)(2,1)} %all-gather.3.cloned.1.call-done), kind=kOutput, calls=%fused_computation.7 | convolution fusion | flops 469827584 | bytes 3801088 | tf_op jit(solution)/shard_map/dot_general | solution.py:23
  40.9 0.0 copy-start.2
  40.9 14.4 %all_gather.17 = bf16[256,1024]{1,0:T(8,128)(2,1)S(1)} all-gather(bf16[256,256]{1,0:T(8,128)(2,1)S(1)} %convolution_convert_fusion.1), channel_id=1, replica_groups=mesh['dp'=8,'tp'=4] {'tp'}, dimensions={1}, use_global_device_ids=true | all-gather | bytes 655360 | tf_op jit(solution)/shard_map/all_gather | solution.py:25
  55.3 0.7 pad_maximum_fusion
  56.0 0.0 all-gather.5.cloned.1.call-update
  56.0 0.0 reduce-scatter.4.cloned.1.call-start
  56.0 0.0 copy-done.3
  56.0 0.2 reduce-window.8
  56.2 0.1 convert_reduce_fusion
  56.3 0.1 convert_reduce_fusion.1
  56.4 0.0 copy-done.1
  56.4 19.8 %all_gather.15 = bf16[3584,128]{1,0:T(8,128)(2,1)} all-gather(bf16[448,128]{1,0:T(8,128)(2,1)S(1)} %copy-done.1), channel_id=1, replica_groups=mesh['dp'=8,'tp'=4] {'dp'}, dimensions={0}, use_global_device_ids=true | all-gather | bytes 1032192 | tf_op jit(solution)/shard_map/all_gather | solution.py:19
  76.2 0.0 copy-done.2
  76.2 16.4 %all_gather.19 = bf16[128,3584]{0,1:T(8,128)(2,1)S(1)} all-gather(bf16[128,448]{0,1:T(8,128)(2,1)S(1)} %copy-done.2), channel_id=1, replica_groups=mesh['dp'=8,'tp'=4] {'dp'}, dimensions={1}, use_global_device_ids=true | all-gather | bytes 1032192 | tf_op jit(solution)/shard_map/all_gather | solution.py:54
  92.6 0.0 all-gather.5.cloned.1.call-done
  92.6 3.8 %select_reduce_fusion = (f32[256]{0:T(256)S(1)}, f32[256,2048]{1,0:T(8,128)}) fusion(s32[256]{0:T(256)S(1)} %iota_add_fusion, s32[2048]{0:T(1024)S(1)} %convert_reduce_fusion, s32[256]{0:T(256)S(1)} %convert_reduce_fusion.1, bf16[2048,256]{1,0:T(8,128)(2,1)} %all-gather.5.cloned.1.call-done, bf16[256,3584]{1,0:T(8,128)(2,1)S(1)} %copy-done, ...), kind=kOutput, calls=%fused_computation.2 | convolution fusion | flops 371785472 | bytes 5385216 | tf_op jit(solution)/shard_map/dot_general | solution.py:41
  96.4 2.3 %fusion.1 = f32[256]{0:T(256)S(1)} fusion(f32[256,2048]{1,0:T(8,128)} %get-tuple-element.8, f32[256]{0:T(256)S(1)} %broadcast_maximum_fusion, s32[256]{0:T(256)S(1)} %iota_add_fusion, s32[2048]{0:T(1024)S(1)} %convert_reduce_fusion, s32[256]{0:T(256)S(1)} %convert_reduce_fusion.1), kind=kLoop, calls=%fused_computation.5 | loop fusion | flops 3145472 | bytes 2109440 | tf_op jit(solution)/shard_map/reduce_sum | solution.py:49
  98.7 4.2 %convolution_convert_fusion = bf16[256,3584]{1,0:T(8,128)(2,1)} fusion(bf16[128,3584]{0,1:T(8,128)(2,1)S(1)} %all_gather.19, f32[256,2048]{1,0:T(8,128)} %get-tuple-element.8, f32[256]{0:T(256)S(1)} %broadcast_maximum_fusion, s32[256]{0:T(256)S(1)} %iota_add_fusion, s32[2048]{0:T(1024)S(1)} %convert_reduce_fusion, s32[256]{0:T(256)S(1)} %convert_reduce_fusion.1, ...), kind=kOutput, calls=%fused_computation | convolution fusion | flops 373227520 | bytes 5386240 | tf_op jit(solution)/shard_map/dot_general | solution.py:52
  102.9 3.8 %copy.6 = bf16[256,3584]{0,1:T(8,128)(2,1)} copy(bf16[256,3584]{1,0:T(8,128)(2,1)} %convolution_convert_fusion) | data formatting | bytes 3670016
  106.8 0.0 reduce-scatter.4.cloned.1.call-update
  106.8 31.4 %reduce-scatter.4.cloned.1.call-done = bf16[896,256]{1,0:T(8,128)(2,1)} async-done(((bf16[3584,256]{1,0:T(8,128)(2,1)}), bf16[896,256]{1,0:T(8,128)(2,1)}) %reduce-scatter.4.cloned.1.call-update) | async-done | bytes 458768
  138.2 2.0 %copy.7 = bf16[256,896]{1,0:T(8,128)(2,1)} copy(bf16[256,896]{0,1:T(8,128)(2,1)} %bitcast.10) | data formatting | bytes 917504
  (3 shorter events, 0.0 us)
Async XLA Ops:
  6.5 32.2 %copy-start = (bf16[256,3584]{1,0:T(8,128)(2,1)S(1)}, bf16[256,3584]{1,0:T(8,128)(2,1)}, u32[]{:S(2)}) copy-start(bf16[256,3584]{1,0:T(8,128)(2,1)} %param.5) | copy-start | bytes 5505028
  6.5 32.2 %all-gather.3.cloned.1.call-start = ((), (), s32[]{:S(2)}) async-start(), calls=%async_computation.1 | async-start | bytes 2064384 | tf_op jit(solution)/shard_map/all_gather | solution.py:20
  7.3 85.4 %all-gather.5.cloned.1.call-start = ((), (), s32[]{:S(2)}) async-start(), calls=%async_computation.2 | async-start | bytes 1179648 | tf_op jit(solution)/shard_map/all_gather | solution.py:36
  7.3 48.7 %copy-start.3 = (s32[4]{0:T(128)S(1)}, s32[4]{0:T(128)}, u32[]{:S(2)}) copy-start(s32[4]{0:T(128)} %param.6) | copy-start | bytes 52
  7.3 49.1 %copy-start.1 = (bf16[448,128]{1,0:T(8,128)(2,1)S(1)}, bf16[448,128]{1,0:T(8,128)(2,1)}, u32[]{:S(2)}) copy-start(bf16[448,128]{1,0:T(8,128)(2,1)} %param.7) | copy-start | bytes 344068
  40.9 35.3 %copy-start.2 = (bf16[128,448]{0,1:T(8,128)(2,1)S(1)}, bf16[128,448]{0,1:T(8,128)(2,1)}, u32[]{:S(2)}) copy-start(bf16[128,448]{0,1:T(8,128)(2,1)} %param.9) | copy-start | bytes 344068
  56.0 82.2 %reduce-scatter.4.cloned.1.call-start = ((), (), s32[]{:S(2)}) async-start(), calls=%async_computation.3 | async-start | bytes 2293760
Sparse Core Ops, SparseCore 0:
  9.0 29.6 all-gather.2
  56.1 23.8 all-gather.4
  106.9 31.2 reduce-scatter.3
where the time goes:
time: 147 us
  waiting for transfers between devices  63.6 us (43%)
  blocking collectives  50.6 us (34%)
  between operations  13.2 us (9%)
  matrix products  10.1 us (7%)
  local copies, waits for them, and re-layouts  5.87 us (4%)
  other arithmetic  3.38 us (2%)
    unnamed x4, waiting for transfers between devices  32.2 us
    all_gather x1, waiting for transfers between devices, body(): lax.all_gather(w_keyval, 'dp', axis=0, tiled=True)  31.4 us
    all_gather x1, blocking collectives, body(): lax.all_gather(w_query, 'dp', axis=0, tiled=True)  19.8 us
    all_gather x1, blocking collectives, body(): lax.all_gather(w_out, 'dp', axis=1, tiled=True)  16.4 us
    all_gather x1, blocking collectives, body(): lax.all_gather(keyval_sum.astype(jnp.bfloat16), 'tp', axis=1, tiled=True)  14.4 us
    unnamed x10, local copies, waits for them, and re-layouts  5.84 us
    dot_general x1, matrix products, body(): jnp.dot(heads_out, lax.all_gather(w_out, 'dp', axis=1, tiled=True), prefe...  4.21 us
    dot_general x1, matrix products, body(): jnp.dot(query, pieces[:, :HD].T, preferred_element_type=jnp.float32)  3.75 us
  transfers between devices with their start and end apart: 3, of which 2 were waited for; matrix products, arithmetic and copies ran while one was open for 0% of the time, Pallas kernels for 0%

commit v1 on v0

--- a/solution.py
+++ b/solution.py
@@ -22,7 +22,9 @@
     query_sum = jnp.dot(hidden_states, pieces[0], preferred_element_type=jnp.float32)
     keyval_sum = jnp.dot(hidden_states, pieces[1], preferred_element_type=jnp.float32)
     query = (query_sum * head_scale).astype(jnp.bfloat16)
-    keyval = lax.all_gather(keyval_sum.astype(jnp.bfloat16), "tp", axis=1, tiled=True)
+    part = keyval_sum.astype(jnp.bfloat16)
+    blocks = lax.all_gather(part, "tp")
+    keyval = jnp.concatenate(blocks, axis=1)
     kv_count = keyval.shape[1] // (2 * HD)
     per_group = lax.axis_size("tp") // kv_count
     kv_head = lax.axis_index("tp") // per_group

time: 147 us -> 143 us (0.973)
  blocking collectives: 50.6 us -> 44.9 us
    all_gather x1, blocking collectives: 14.4 us -> 10.1 us  [body(): blocks = lax.all_gather(part, 'tp')]
where the time goes in v1:
time: 143 us
  waiting for transfers between devices  65 us (45%)
  blocking collectives  44.9 us (31%)
  between operations  13.2 us (9%)
  matrix products  10.4 us (7%)
  local copies, waits for them, and re-layouts  6.06 us (4%)
  other arithmetic  3.37 us (2%)
    unnamed x4, waiting for transfers between devices  33.6 us
    all_gather x1, waiting for transfers between devices, body(): lax.all_gather(w_keyval, 'dp', axis=0, tiled=True)  31.4 us
    all_gather x1, blocking collectives, body(): lax.all_gather(w_query, 'dp', axis=0, tiled=True)  18.8 us
    all_gather x1, blocking collectives, body(): lax.all_gather(w_out, 'dp', axis=1, tiled=True)  15.9 us
    all_gather x1, blocking collectives, body(): blocks = lax.all_gather(part, 'tp')  10.1 us
    unnamed x10, local copies, waits for them, and re-layouts  5.84 us
    dot_general x1, matrix products, body(): jnp.dot(heads_out, lax.all_gather(w_out, 'dp', axis=1, tiled=True), prefe...  4.51 us
    dot_general x1, matrix products, body(): jnp.dot(query, pieces[:, :HD].T, preferred_element_type=jnp.float32)  3.78 us
  transfers between devices with their start and end apart: 3, of which 2 were waited for; matrix products, arithmetic and copies ran while one was open for 0% of the time, Pallas kernels for 0%

profile of v1, /device:TPU:0, one launch (start us, length us, event | category | flops | bytes accessed | tf_op | source)
XLA Modules:
  0.0 143.1 jit_solution(15164330954555595961)
XLA Ops:
  6.5 0.0 copy-start
  6.5 0.0 all-gather.4.cloned.1.call-start
  6.5 0.7 all-gather.4.cloned.1.call-update
  7.3 0.0 all-gather.6.cloned.1.call-start
  7.3 31.4 %all-gather.4.cloned.1.call-done = bf16[3584,256]{1,0:T(8,128)(2,1)} async-done(((bf16[448,256]{1,0:T(8,128)(2,1)}), bf16[3584,256]{1,0:T(8,128)(2,1)}) %all-gather.4.cloned.1.call-update) | async-done | bytes 1835024 | tf_op jit(solution)/shard_map/all_gather | solution.py:20
  38.7 0.0 copy-done
  38.7 2.1 %convolution_convert_fusion.1 = bf16[256,256]{1,0:T(8,128)(2,1)S(1)} fusion(bf16[256,3584]{1,0:T(8,128)(2,1)S(1)} %copy-done, bf16[3584,256]{1,0:T(8,128)(2,1)} %all-gather.4.cloned.1.call-done), kind=kOutput, calls=%fused_computation.7 | convolution fusion | flops 469827584 | bytes 3801088 | tf_op jit(solution)/shard_map/dot_general | solution.py:23
  40.9 0.0 copy-start.3
  40.9 0.0 copy-start.1
  40.9 0.0 copy-start.2
  40.9 10.1 %all-gather = bf16[1024,256]{1,0:T(8,128)(2,1)S(1)} all-gather(bf16[256,256]{1,0:T(8,128)(2,1)S(1)} %convolution_convert_fusion.1), channel_id=2, replica_groups=mesh['dp'=8,'tp'=4] {'tp'}, dimensions={0}, use_global_device_ids=true | all-gather | bytes 655360 | tf_op jit(solution)/shard_map/all_gather | solution.py:26
  51.0 0.2 copy.8
  51.3 0.7 pad_maximum_fusion
  51.9 0.0 all-gather.6.cloned.1.call-update
  51.9 0.0 reduce-scatter.4.cloned.1.call-start
  52.0 0.0 copy-done.3
  52.0 0.2 reduce-window.8
  52.2 0.1 convert_reduce_fusion
  52.3 0.1 convert_reduce_fusion.1
  52.4 0.0 copy-done.1
  52.4 18.8 %all_gather.18 = bf16[3584,128]{1,0:T(8,128)(2,1)} all-gather(bf16[448,128]{1,0:T(8,128)(2,1)S(1)} %copy-done.1), channel_id=1, replica_groups=mesh['dp'=8,'tp'=4] {'dp'}, dimensions={0}, use_global_device_ids=true | all-gather | bytes 1032192 | tf_op jit(solution)/shard_map/all_gather | solution.py:19
  71.2 0.0 copy-done.2
  71.2 15.9 %all_gather.23 = bf16[128,3584]{0,1:T(8,128)(2,1)S(1)} all-gather(bf16[128,448]{0,1:T(8,128)(2,1)S(1)} %copy-done.2), channel_id=1, replica_groups=mesh['dp'=8,'tp'=4] {'dp'}, dimensions={1}, use_global_device_ids=true | all-gather | bytes 1032192 | tf_op jit(solution)/shard_map/all_gather | solution.py:56
  87.2 0.0 all-gather.6.cloned.1.call-done
  87.2 3.8 %select_reduce_fusion = (f32[256]{0:T(256)S(1)}, f32[256,2048]{1,0:T(8,128)}) fusion(s32[256]{0:T(256)S(1)} %iota_add_fusion, s32[2048]{0:T(1024)S(1)} %convert_reduce_fusion, s32[256]{0:T(256)S(1)} %convert_reduce_fusion.1, bf16[2048,256]{0,1:T(8,128)(2,1)} %all-gather.6.cloned.1.call-done, bf16[256,3584]{1,0:T(8,128)(2,1)S(1)} %copy-done, ...), kind=kOutput, calls=%fused_computation.2 | convolution fusion | flops 371785472 | bytes 5385216 | tf_op jit(solution)/shard_map/dot_general | solution.py:43
  90.9 2.3 %fusion.1 = f32[256]{0:T(256)S(1)} fusion(f32[256,2048]{1,0:T(8,128)} %get-tuple-element.8, f32[256]{0:T(256)S(1)} %broadcast_maximum_fusion, s32[256]{0:T(256)S(1)} %iota_add_fusion, s32[2048]{0:T(1024)S(1)} %convert_reduce_fusion, s32[256]{0:T(256)S(1)} %convert_reduce_fusion.1), kind=kLoop, calls=%fused_computation.5 | loop fusion | flops 3145472 | bytes 2109440 | tf_op jit(solution)/shard_map/reduce_sum | solution.py:51
  93.3 4.5 %convolution_convert_fusion = bf16[256,3584]{1,0:T(8,128)(2,1)} fusion(bf16[128,3584]{0,1:T(8,128)(2,1)S(1)} %all_gather.23, f32[256,2048]{1,0:T(8,128)} %get-tuple-element.8, f32[256]{0:T(256)S(1)} %broadcast_maximum_fusion, s32[256]{0:T(256)S(1)} %iota_add_fusion, s32[2048]{0:T(1024)S(1)} %convert_reduce_fusion, s32[256]{0:T(256)S(1)} %convert_reduce_fusion.1, ...), kind=kOutput, calls=%fused_computation | convolution fusion | flops 373227520 | bytes 5386240 | tf_op jit(solution)/shard_map/dot_general | solution.py:54
  97.8 3.8 %copy.9 = bf16[256,3584]{0,1:T(8,128)(2,1)} copy(bf16[256,3584]{1,0:T(8,128)(2,1)} %convolution_convert_fusion) | data formatting | bytes 3670016
  101.6 0.0 reduce-scatter.4.cloned.1.call-update
  101.6 32.9 %reduce-scatter.4.cloned.1.call-done = bf16[896,256]{1,0:T(8,128)(2,1)} async-done(((bf16[3584,256]{1,0:T(8,128)(2,1)}), bf16[896,256]{1,0:T(8,128)(2,1)}) %reduce-scatter.4.cloned.1.call-update) | async-done | bytes 458768
  134.5 2.0 %copy.10 = bf16[256,896]{1,0:T(8,128)(2,1)} copy(bf16[256,896]{0,1:T(8,128)(2,1)} %bitcast.16) | data formatting | bytes 917504
  (3 shorter events, 0.0 us)
Async XLA Ops:
  6.5 32.2 %copy-start = (bf16[256,3584]{1,0:T(8,128)(2,1)S(1)}, bf16[256,3584]{1,0:T(8,128)(2,1)}, u32[]{:S(2)}) copy-start(bf16[256,3584]{1,0:T(8,128)(2,1)} %param.5) | copy-start | bytes 5505028
  6.5 32.2 %all-gather.4.cloned.1.call-start = ((), (), s32[]{:S(2)}) async-start(), calls=%async_computation.1 | async-start | bytes 2064384 | tf_op jit(solution)/shard_map/all_gather | solution.py:20
  7.3 79.9 %all-gather.6.cloned.1.call-start = ((), (), s32[]{:S(2)}) async-start(), calls=%async_computation.2 | async-start | bytes 1179648 | tf_op jit(solution)/shard_map/all_gather | solution.py:38
  40.9 11.1 %copy-start.3 = (s32[4]{0:T(128)S(1)}, s32[4]{0:T(128)}, u32[]{:S(2)}) copy-start(s32[4]{0:T(128)} %param.6) | copy-start | bytes 52
  40.9 11.5 %copy-start.1 = (bf16[448,128]{1,0:T(8,128)(2,1)S(1)}, bf16[448,128]{1,0:T(8,128)(2,1)}, u32[]{:S(2)}) copy-start(bf16[448,128]{1,0:T(8,128)(2,1)} %param.7) | copy-start | bytes 344068
  40.9 30.4 %copy-start.2 = (bf16[128,448]{0,1:T(8,128)(2,1)S(1)}, bf16[128,448]{0,1:T(8,128)(2,1)}, u32[]{:S(2)}) copy-start(bf16[128,448]{0,1:T(8,128)(2,1)} %param.9) | copy-start | bytes 344068
  51.9 82.6 %reduce-scatter.4.cloned.1.call-start = ((), (), s32[]{:S(2)}) async-start(), calls=%async_computation.3 | async-start | bytes 2293760
Sparse Core Ops, SparseCore 0:
  9.0 29.6 all-gather.3
  52.1 24.8 all-gather.5
  101.8 32.7 reduce-scatter.3
